TPU v7x, 32 devices: a whole 2x2x4 slice. The times are simulated.
32 devices in a mesh: shot: 4 (over x, core), tile: 8 (over z, y).
Axes of the slice: x: 2, y: 2, z: 4, core: 2. Of those that a mesh axis runs over, the one named last changes fastest.
Arguments:
- partials: bfloat16 [32, 8, 512, 512], P(('shot', 'tile')), may hold values from -6 to 6
Outputs:
- filtered: float32 [8, 512, 512], P('shot', 'tile')
All inputs are finite; a program needn't handle non-finite values.
Results may differ from a plain program's by a relative error of at most 0.0003.
Values may be sent and summed in bfloat16 or wider, within the bound.
A program may use at most 64 MiB of HBM per device.

v0:
```python
import functools

import jax
import jax.numpy as jnp
from jax import lax
from jax.experimental import pallas as pl
from jax.experimental.pallas import tpu as pltpu
from jax.sharding import PartitionSpec as P

MESH = pl.DeviceIdType.MESH
F32 = jnp.float32


def kernel(groups, members, src, out, own_a, own_b, own_c, r1a, r1b, s1a, s1b, r2a, r2b,
           s2, r3, s3, r4, rz, sc, rc, tc, rd, img, low, high, top, bottom, own_sem,
           p1s, p1r, q1s, q1r, p2s, p2r, p3s, p3r, zs, zr, cs, cr, ds, dr, hs, hr):
    nd, nz, rows, width = src.shape[2], src.shape[3], src.shape[5], src.shape[6]
    cw = width // 4
    rr = s2.shape[3]
    parts = rows // rr
    edge = top.shape[1]
    units = [(j, d, h * rr) for j in range(2) for d in range(nd) for h in range(parts)]
    crows = own_c.shape[4]
    c_unit = (1, nd - 1, rows - crows)
    cj, cd, ch = c_unit
    units = units[: len(units) - crows // rr]
    steps = len(units)
    g, t = lax.axis_index("shot"), lax.axis_index("tile")
    x, c = g // 2, g % 2
    z, y = t // 2, t % 2

    def dev(gx, tx):
        return {"shot": gx, "tile": tx}

    x_peer = dev((1 - x) * 2 + c, t)
    c_peer = dev(x * 2 + 1 - c, t)
    y_peer = dev(g, z * 2 + 1 - y)
    d_peer = dev((1 - x) * 2 + c, z * 2 + 1 - y)

    def z_peer(o):
        return dev(g, lax.rem(z + o, nz) * 2 + y)

    beside = [
        (g > 0, dev(g - 1, t)),
        (g < groups - 1, dev(g + 1, t)),
        (t > 0, dev(g, t - 1)),
        (t < members - 1, dev(g, t + 1)),
    ]

    def col(kind, j):
        return pl.ds((2 * kind + j) * cw, cw)

    def row(h):
        return pl.ds(h, rr)

    c_row = pl.ds(ch, crows)

    barrier = pltpu.get_barrier_semaphore()
    peers = [x_peer, c_peer, y_peer, d_peer] + [z_peer(o) for o in range(1, nz)]
    count = jnp.int32(len(peers))
    for peer in peers:
        pl.semaphore_signal(barrier, inc=1, device_id=peer, device_id_type=MESH)
    for there, peer in beside:
        count = count + jnp.where(there, 1, 0)

        @pl.when(there)
        def _():
            pl.semaphore_signal(barrier, inc=1, device_id=peer, device_id_type=MESH)
    loads = [
        pltpu.make_async_copy(src.at[x, :, :, :, :, :, pl.ds(0, 2 * cw)], own_a, own_sem.at[0]),
        pltpu.make_async_copy(src.at[:, :, :, :, y, :, pl.ds(2 * cw, 2 * cw)], own_b, own_sem.at[1]),
    ]
    for kind in range(2):
        loads.append(pltpu.make_async_copy(src.at[:, :, cd, z, :, c_row, col(kind, cj)],
                                           own_c.at[kind], own_sem.at[2 + kind]))
    for copy in loads:
        copy.start()
    pl.semaphore_wait(barrier, count)

    def remote(a, b, s, r, peer):
        copy = pltpu.make_async_remote_copy(
            src_ref=a, dst_ref=b, send_sem=s, recv_sem=r, device_id=peer, device_id_type=MESH
        )
        copy.start()
        return copy

    def done(ref, sem):
        pltpu.make_async_copy(ref, ref, sem).wait()

    first, second, third, fourth = {}, {}, {}, {}

    def p1(k):
        j, d, h = units[k]
        first[k] = (
            remote(src.at[1 - x, :, d, :, :, row(h), col(0, j)], r1a.at[k],
                   p1s.at[0], p1r.at[0, k], x_peer),
            remote(src.at[:, :, d, :, 1 - y, row(h), col(1, j)], r1b.at[k],
                   p1s.at[1], p1r.at[1, k], y_peer),
        )

    def two_a(k, core, side):
        j, d, h = units[k]
        own = own_a[core, d, :, side, row(h), pl.ds(j * cw, cw)]
        return own.astype(F32) + r1a[k, core, :, side].astype(F32)

    def two_b(k, core, side):
        j, d, h = units[k]
        own = own_b[side, core, d, :, row(h), pl.ds(j * cw, cw)]
        return own.astype(F32) + r1b[k, side, core].astype(F32)

    def q1(k):
        a, b = first[k]
        a.wait_recv()
        for side in range(2):
            s1a[k, side] = two_a(k, 1 - c, side)
        ca = remote(s1a.at[k], r2a.at[k], q1s.at[0], q1r.at[0, k], c_peer)
        b.wait_recv()
        for side in range(2):
            s1b[k, side] = two_b(k, 1 - c, side)
        cb = remote(s1b.at[k], r2b.at[k], q1s.at[1], q1r.at[1, k], c_peer)
        second[k] = (ca, cb)

    def p2(k):
        a, b = second[k]
        a.wait_recv()
        s2[0, k] = two_a(k, c, 1 - y) + r2a[k, 1 - y]
        ca = remote(s2.at[0, k], r3.at[0, k], p2s.at[0], p2r.at[0, k], y_peer)
        b.wait_recv()
        s2[1, k] = two_b(k, c, 1 - x) + r2b[k, 1 - x]
        cb = remote(s2.at[1, k], r3.at[1, k], p2s.at[1], p2r.at[1, k], x_peer)
        third[k] = (ca, cb)

    def p3(k):
        copies = []
        for kind in range(2):
            third[k][kind].wait_recv()
            if kind == 0:
                s3[0, k] = two_a(k, c, y) + r2a[k, y] + r3[0, k]
            else:
                s3[1, k] = two_b(k, c, x) + r2b[k, x] + r3[1, k]
            for o in range(1, nz):
                to = lax.rem(z + o, nz)
                copies.append(remote(s3.at[kind, k, to], r4.at[kind, k, z],
                                     p3s.at[kind], p3r.at[kind, k], z_peer(o)))
        fourth[k] = copies

    z_first, z_core, z_last = [], [], []

    def c_z():
        for kind in range(2):
            for o in range(1, nz):
                to = lax.rem(z + o, nz)
                z_first.append(remote(src.at[:, :, cd, to, :, c_row, col(kind, cj)], rz.at[kind, o - 1],
                                      zs.at[kind], zr.at[kind], z_peer(o)))

    def c_sum(kind, core, side):
        total = own_c[kind, side, core].astype(F32)
        for o in range(1, nz):
            total = total + rz[kind, o - 1, side, core].astype(F32)
        return total

    def c_core():
        for kind in range(2):
            done(rz.at[kind], zr.at[kind])
            for side in range(2):
                sc[kind, side] = c_sum(kind, 1 - c, side)
            z_core.append(remote(sc.at[kind], rc.at[kind], cs.at[kind], cr.at[kind], c_peer))

    def c_xy():
        for kind in range(2):
            z_core[kind].wait_recv()
            for side in range(2):
                tc[kind, side] = c_sum(kind, c, side) + rc[kind, side]
            for i, (a, b, peer) in enumerate(
                [(1 - x, 1 - y, d_peer), (1 - x, y, x_peer), (x, 1 - y, y_peer)]
            ):
                z_last.append(remote(tc.at[kind, a, b], rd.at[kind, i], ds.at[kind], dr.at[kind], peer))

    scale = 1.0 / jnp.sqrt(F32(groups * members))

    def halo(side, a, b):
        there, peer = beside[side]

        @pl.when(there)
        def _():
            remote(a, b, hs.at[side], hr.at[side], peer)

    def finish(kind, unit, total):
        j, d, h = unit
        cols = col(kind, j)
        span = pl.ds(h, total.shape[0])
        img[d, span, cols] = total * scale
        if d == 0:
            halo(0, img.at[d, span, cols], high.at[span, cols])
        if d == nd - 1:
            halo(1, img.at[d, span, cols], low.at[span, cols])
        if h == 0:
            halo(2, img.at[d, pl.ds(0, edge), cols], bottom.at[d, :, cols])
        if h + total.shape[0] == rows:
            halo(3, img.at[d, pl.ds(rows - edge, edge), cols], top.at[d, :, cols])

    def last(k):
        for kind in range(2):
            total = s3[kind, k, z]
            done(r4.at[kind, k, pl.ds(0, nz - 1)], p3r.at[kind, k])
            for o in range(1, nz):
                total = total + r4[kind, k, lax.rem(z + nz - o, nz)]
            finish(kind, units[k], total)

    def c_last():
        for kind in range(2):
            total = tc[kind, x, y]
            done(rd.at[kind], dr.at[kind])
            for i in range(3):
                total = total + rd[kind, i]
            finish(kind, c_unit, total)

    ahead, lag2, lag3, lag4 = 3, 0, 3, 7
    at_core = min(6, steps - 1)
    at_xy = max(steps - 2, at_core)
    p1(0)
    c_z()
    for k in range(1, min(ahead, steps)):
        p1(k)
    for copy in loads:
        copy.wait()
    for k in range(steps + lag4):
        if k < steps:
            q1(k)
        if 0 <= k - lag2 < steps:
            p2(k - lag2)
        if k + ahead < steps:
            p1(k + ahead)
        if 0 <= k - lag3 < steps:
            p3(k - lag3)
        if k == at_core:
            c_core()
        if k == at_xy:
            c_xy()
        if k == steps + lag4 - 1:
            c_last()
        if 0 <= k - lag4 < steps:
            last(k - lag4)
    for side, ref in enumerate([high, low, bottom, top]):
        @pl.when(beside[side ^ 1][0])
        def _():
            done(ref, hr.at[side])

    rown = lax.broadcasted_iota(jnp.int32, (rows, width), 0)
    coln = lax.broadcasted_iota(jnp.int32, (rows, width), 1)
    for d in range(nd):
        here = img[d]
        below = img[d - 1] if d > 0 else jnp.where(g > 0, low[...], 0.0)
        above = img[d + 1] if d < nd - 1 else jnp.where(g < groups - 1, high[...], 0.0)
        before = jnp.where(t > 0, top[d, edge - 1:edge, :], 0.0)
        after = jnp.where(t < members - 1, bottom[d, 0:1, :], 0.0)
        near = above + below
        near = near + jnp.where(rown == rows - 1, after, pltpu.roll(here, rows - 1, 0))
        near = near + jnp.where(rown == 0, before, pltpu.roll(here, 1, 0))
        near = near + jnp.where(coln == width - 1, 0.0, pltpu.roll(here, width - 1, 1))
        near = near + jnp.where(coln == 0, 0.0, pltpu.roll(here, 1, 1))
        out[d] = 6.0 * here - near
    for side, ref in enumerate([high, low, bottom, top]):
        @pl.when(beside[side][0])
        def _():
            done(ref, hs.at[side])
    for kind, (one, two) in enumerate([(r1a, r2a), (r1b, r2b)]):
        done(one, p1s.at[kind])
        done(two, q1s.at[kind])
        done(r3.at[kind], p2s.at[kind])
        done(r4.at[kind, :, pl.ds(0, nz - 1)], p3s.at[kind])
        done(rz.at[kind], zs.at[kind])
        done(rc.at[kind], cs.at[kind])
        done(rd.at[kind], ds.at[kind])


def body(groups, members, partials):
    shots, depth, lateral, width = partials.shape
    nd, nz, rows, cw = depth // groups, members // 2, lateral // members, width // 4
    parts = 4 if rows % 64 == 0 else 1
    rr, edge = rows // parts, min(8, rows)
    crows = 2 * rr if parts > 1 else rr
    steps = 2 * nd * parts - crows // rr
    src = partials.reshape(2, 2, nd, nz, 2, rows, width)
    kind = partials.dtype
    dma = pltpu.SemaphoreType.DMA
    return pl.pallas_call(
        functools.partial(kernel, groups, members),
        out_shape=jax.ShapeDtypeStruct((nd, rows, width), F32),
        in_specs=[pl.BlockSpec(memory_space=pl.ANY)],
        out_specs=pl.BlockSpec(memory_space=pltpu.VMEM),
        scratch_shapes=[
            pltpu.VMEM((2, nd, nz, 2, rows, 2 * cw), kind),
            pltpu.VMEM((2, 2, nd, nz, rows, 2 * cw), kind),
            pltpu.VMEM((2, 2, 2, 2, crows, cw), kind),
            pltpu.VMEM((steps, 2, nz, 2, rr, cw), kind),
            pltpu.VMEM((steps, 2, 2, nz, rr, cw), kind),
            pltpu.VMEM((steps, 2, nz, rr, cw), F32),
            pltpu.VMEM((steps, 2, nz, rr, cw), F32),
            pltpu.VMEM((steps, 2, nz, rr, cw), F32),
            pltpu.VMEM((steps, 2, nz, rr, cw), F32),
            pltpu.VMEM((2, steps, nz, rr, cw), F32),
            pltpu.VMEM((2, steps, nz, rr, cw), F32),
            pltpu.VMEM((2, steps, nz, rr, cw), F32),
            pltpu.VMEM((2, steps, nz, rr, cw), F32),
            pltpu.VMEM((2, nz - 1, 2, 2, 2, crows, cw), kind),
            pltpu.VMEM((2, 2, 2, crows, cw), F32),
            pltpu.VMEM((2, 2, 2, crows, cw), F32),
            pltpu.VMEM((2, 2, 2, crows, cw), F32),
            pltpu.VMEM((2, 3, crows, cw), F32),
            pltpu.VMEM((nd, rows, width), F32),
            pltpu.VMEM((rows, width), F32),
            pltpu.VMEM((rows, width), F32),
            pltpu.VMEM((nd, edge, width), F32),
            pltpu.VMEM((nd, edge, width), F32),
            dma((4,)),
            dma((2,)), dma((2, steps)),
            dma((2,)), dma((2, steps)),
            dma((2,)), dma((2, steps)),
            dma((2,)), dma((2, steps)),
            dma((2,)), dma((2,)),
            dma((2,)), dma((2,)),
            dma((2,)), dma((2,)),
            dma((4,)), dma((4,)),
        ],
        compiler_params=pltpu.CompilerParams(collective_id=0, has_side_effects=True),
    )(src)


def solution(mesh):
    groups, members = mesh.shape["shot"], mesh.shape["tile"]
    return jax.shard_map(
        functools.partial(body, groups, members),
        mesh=mesh,
        in_specs=(P(("shot", "tile"), None, None, None),),
        out_specs=P("shot", "tile", None),
        check_vma=False,
    )
```

profile of v0, /device:TPU:0, one launch (start us, length us, event | category | flops | bytes accessed | tf_op | source)
XLA Modules:
  0.0 49.2 jit_solution(1086494748734624092)
XLA Ops:
  0.0 47.5 %shard_map.17 = f32[2,64,512]{2,1,0:T(8,128)} custom-call(bf16[2,2,2,4,2,64,512]{6,5,4,3,2,1,0:T(8,128)(2,1)} %bitcast.1), custom_call_target="tpu_custom_call" | custom-call | tf_op jit(solution)/shard_map/pallas_call | solution.py:287
  47.5 1.7 %copy.3 = f32[2,64,512]{2,1,0:T(8,128)} copy(f32[2,64,512]{2,1,0:T(8,128)} %shard_map.17) | data formatting | bytes 524288
where the time goes:
time: 49.4 us; the launch traced here: 49.2 us
  Pallas kernels  47.5 us (96%)
  local copies, waits for them, and re-layouts  1.67 us (3%)
    pallas_call x1, Pallas kernels, body(): pl.pallas_call(functools.partial(kernel, groups, members), out_shape=jax....  47.5 us
    unnamed x1, local copies, waits for them, and re-layouts  1.67 us

commit v1 on v0

v1 whole, which is shorter than its diff:
```python
import functools

import jax
import jax.numpy as jnp
from jax import lax
from jax.experimental import pallas as pl
from jax.experimental.pallas import tpu as pltpu
from jax.sharding import PartitionSpec as P

MESH = pl.DeviceIdType.MESH
F32 = jnp.float32
TOP = 180.0
TINY = 1e-30


def encode(value, scale):
    w = value * scale
    p = w * w
    p = p * p
    p = p * p
    p = p * p
    return jnp.where(w < 0.0, -p, p).astype(jnp.bfloat16)


def decode(code, scale):
    code = code.astype(F32)
    root = lax.rsqrt(lax.rsqrt(lax.rsqrt(lax.rsqrt(jnp.abs(code))))) * scale
    return jnp.where(code < 0.0, -root, root)


def kernel(groups, members, src, out, own, rp, s1a, s1b, r1a, r1b, s2, r2, s3f, s3, r4,
           lim, lim_c, lim_1, lim_2, lim_3, img, low, high, top, bottom, own_sem,
           cs, cr, p1s, p1r, p2s, p2r, p3s, p3r, ms, mr, ns, nr, hs, hr):
    nd, nz, rows, width = src.shape[2], src.shape[3], src.shape[5], src.shape[6]
    cw = width // 4
    rr = s2.shape[3]
    edge = top.shape[1]
    units = [(j, d, h) for d in range(nd) for h in range(0, rows, rr) for j in range(2)]
    steps = len(units)
    g, t = lax.axis_index("shot"), lax.axis_index("tile")
    x, c = g // 2, g % 2
    z, y = t // 2, t % 2

    def dev(gx, tx):
        return {"shot": gx, "tile": tx}

    x_peer = dev((1 - x) * 2 + c, t)
    c_peer = dev(x * 2 + 1 - c, t)
    y_peer = dev(g, z * 2 + 1 - y)

    def z_peer(o):
        return dev(g, lax.rem(z + o, nz) * 2 + y)

    beside = [
        (g > 0, dev(g - 1, t)),
        (g < groups - 1, dev(g + 1, t)),
        (t > 0, dev(g, t - 1)),
        (t < members - 1, dev(g, t + 1)),
    ]

    barrier = pltpu.get_barrier_semaphore()
    peers = [x_peer, c_peer, y_peer] + [z_peer(o) for o in range(1, nz)]
    count = jnp.int32(len(peers))
    for peer in peers:
        pl.semaphore_signal(barrier, inc=1, device_id=peer, device_id_type=MESH)
    for there, peer in beside:
        count = count + jnp.where(there, 1, 0)

        @pl.when(there)
        def _():
            pl.semaphore_signal(barrier, inc=1, device_id=peer, device_id_type=MESH)
    loads = []
    for d in range(nd):
        for core in range(2):
            i = 2 * d + core
            at = 1 - c if core == 0 else c
            loads.append(pltpu.make_async_copy(src.at[:, at, d], own.at[:, at, d], own_sem.at[i]))
    for copy in loads:
        copy.start()

    def remote(a, b, s, r, peer):
        copy = pltpu.make_async_remote_copy(
            src_ref=a, dst_ref=b, send_sem=s, recv_sem=r, device_id=peer, device_id_type=MESH
        )
        copy.start()
        return copy

    def done(ref, sem):
        pltpu.make_async_copy(ref, ref, sem).wait()

    pair, first, second, third = {}, {}, {}, {}

    def span(k):
        j, d, h = units[k]
        return d, pl.ds(h, rr), pl.ds(2 * j * cw, 2 * cw)

    def kind_cols(kind, k):
        j, d, h = units[k]
        return pl.ds((2 * j + kind) * cw, cw)

    def give(k):
        d, r, w = span(k)
        pair[k] = remote(own.at[:, 1 - c, d, :, :, r, w], rp.at[k], cs.at[0], cr.at[k], c_peer)

    def mine(k, kind, a, b):
        d, r, _ = span(k)
        lanes = pl.ds(kind * cw, cw)
        return own[a, c, d, :, b, r, kind_cols(kind, k)].astype(F32) + rp[k, a, :, b, :, lanes].astype(F32)

    for d in range(nd):
        loads[2 * d].wait()
    pl.semaphore_wait(barrier, count)
    lead = min(4, steps)
    for k in range(lead):
        give(k)
    for d in range(nd):
        loads[2 * d + 1].wait()

    most = None
    for a in range(2):
        for b in range(2):
            for d in range(nd):
                def step(i, most, a=a, b=b, d=d):
                    for e in range(2):
                        block = jnp.abs(own[a, b, d, i, e])
                        for r in range(0, rows, rr):
                            most = jnp.maximum(most, block[r:r + rr])
                    return most
                if most is None:
                    most = jnp.zeros((rr, width), own.dtype)
                most = lax.fori_loop(0, nz, step, most)
    most = jnp.max(most.astype(F32), axis=0, keepdims=True)
    most = jnp.max(most, axis=1, keepdims=True)
    lim[0] = jnp.broadcast_to(jnp.maximum(most, TINY), (rr, cw))
    to_core = remote(lim.at[0], lim_c, ms.at[0], mr.at[0], c_peer)
    for k in range(lead, steps):
        give(k)
    to_core.wait_recv()
    lim[1] = lim[0] + lim_c[...]
    remote(lim.at[1], lim_1.at[0], ms.at[1], mr.at[1], x_peer)
    remote(lim.at[1], lim_1.at[1], ms.at[2], mr.at[2], y_peer)

    def limits(stage):
        if stage == 2:
            for kind, peer in enumerate([y_peer, x_peer]):
                done(lim_1.at[kind], mr.at[1 + kind])
                lim[2 + kind] = lim[1] + lim_1[kind]
                remote(lim.at[2 + kind], lim_2.at[kind], ms.at[3 + kind], mr.at[3 + kind], peer)
        if stage == 3:
            for kind in range(2):
                done(lim_2.at[kind], mr.at[3 + kind])
                lim[4 + kind] = lim[2 + kind] + lim_2[kind]
                for o in range(1, nz):
                    remote(lim.at[4 + kind], lim_3.at[kind, z], ns.at[kind], nr.at[kind], z_peer(o))
        if stage == 4:
            for kind in range(2):
                done(lim_3.at[kind, pl.ds(0, nz - 1)], nr.at[kind])

    def up(ref):
        return (TOP / ref)[None]

    def down(ref):
        return (ref * (1.0 / TOP))[None]

    def p1(k):
        pair[k].wait_recv()
        scale = up(lim[1])
        for b in range(2):
            s1a[k, :, b] = encode(mine(k, 0, 1 - x, b), scale)
        ca = remote(s1a.at[k], r1a.at[k], p1s.at[0], p1r.at[0, k], x_peer)
        for a in range(2):
            s1b[k, a] = encode(mine(k, 1, a, 1 - y), scale)
        cb = remote(s1b.at[k], r1b.at[k], p1s.at[1], p1r.at[1, k], y_peer)
        first[k] = (ca, cb)

    def p2(k):
        a, b = first[k]
        a.wait_recv()
        s2[0, k] = encode(mine(k, 0, x, 1 - y) + decode(r1a[k, :, 1 - y], down(lim_1[0])), up(lim[2]))
        ca = remote(s2.at[0, k], r2.at[0, k], p2s.at[0], p2r.at[0, k], y_peer)
        b.wait_recv()
        s2[1, k] = encode(mine(k, 1, 1 - x, y) + decode(r1b[k, 1 - x], down(lim_1[1])), up(lim[3]))
        cb = remote(s2.at[1, k], r2.at[1, k], p2s.at[1], p2r.at[1, k], x_peer)
        second[k] = (ca, cb)

    def p3(k):
        for kind in range(2):
            lanes = pl.ds(kind * cw, cw)
            if kind == 0:
                total = mine(k, 0, x, y) + decode(r1a[k, :, y], down(lim_1[0]))
            else:
                total = mine(k, 1, x, y) + decode(r1b[k, x], down(lim_1[1]))
            second[k][kind].wait_recv()
            total = total + decode(r2[kind, k], down(lim_2[kind]))
            s3f[k, :, :, lanes] = total
            s3[k, :, :, lanes] = encode(total, up(lim[4 + kind]))
        copies = []
        for o in range(1, nz):
            to = lax.rem(z + o, nz)
            copies.append(remote(s3.at[k, to], r4.at[k, z], p3s.at[0], p3r.at[k], z_peer(o)))
        third[k] = copies

    shrink = 1.0 / jnp.sqrt(F32(groups * members))

    def halo(side, a, b):
        there, peer = beside[side]

        @pl.when(there)
        def _():
            remote(a, b, hs.at[side], hr.at[side], peer)

    def last(k):
        j, d, h = units[k]
        _, r, w = span(k)
        done(r4.at[k, pl.ds(0, nz - 1)], p3r.at[k])
        for kind in range(2):
            lanes = pl.ds(kind * cw, cw)
            total = s3f[k, z, :, lanes]
            for o in range(1, nz):
                at = lax.rem(z + nz - o, nz)
                total = total + decode(r4[k, at, :, lanes], lim_3[kind, at] * (1.0 / TOP))
            img[d, r, kind_cols(kind, k)] = total * shrink
        if d == 0:
            halo(0, img.at[d, r, w], high.at[r, w])
        if d == nd - 1:
            halo(1, img.at[d, r, w], low.at[r, w])
        if h == 0:
            halo(2, img.at[d, pl.ds(0, edge), w], bottom.at[d, :, w])
        if h + rr == rows:
            halo(3, img.at[d, pl.ds(rows - edge, edge), w], top.at[d, :, w])

    ahead, lag3, lag4 = 3, 2, 5
    for k in range(min(ahead, steps)):
        p1(k)
    limits(2)
    for k in range(steps + lag4):
        if k < steps:
            p2(k)
        if k + ahead < steps:
            p1(k + ahead)
        if k == min(1, steps - 1):
            limits(3)
        if 0 <= k - lag3 < steps:
            p3(k - lag3)
        if k == lag4:
            limits(4)
        if 0 <= k - lag4 < steps:
            last(k - lag4)
    for side, ref in enumerate([high, low, bottom, top]):
        @pl.when(beside[side ^ 1][0])
        def _():
            done(ref, hr.at[side])

    rown = lax.broadcasted_iota(jnp.int32, (rows, width), 0)
    coln = lax.broadcasted_iota(jnp.int32, (rows, width), 1)
    for d in range(nd):
        here = img[d]
        below = img[d - 1] if d > 0 else jnp.where(g > 0, low[...], 0.0)
        above = img[d + 1] if d < nd - 1 else jnp.where(g < groups - 1, high[...], 0.0)
        before = jnp.where(t > 0, top[d, edge - 1:edge, :], 0.0)
        after = jnp.where(t < members - 1, bottom[d, 0:1, :], 0.0)
        near = above + below
        near = near + jnp.where(rown == rows - 1, after, pltpu.roll(here, rows - 1, 0))
        near = near + jnp.where(rown == 0, before, pltpu.roll(here, 1, 0))
        near = near + jnp.where(coln == width - 1, 0.0, pltpu.roll(here, width - 1, 1))
        near = near + jnp.where(coln == 0, 0.0, pltpu.roll(here, 1, 1))
        out[d] = 6.0 * here - near
    for side, ref in enumerate([high, low, bottom, top]):
        @pl.when(beside[side][0])
        def _():
            done(ref, hs.at[side])
    done(rp, cs.at[0])
    done(r1a, p1s.at[0])
    done(r1b, p1s.at[1])
    for kind in range(2):
        done(r2.at[kind], p2s.at[kind])
        done(lim_3.at[kind, pl.ds(0, nz - 1)], ns.at[kind])
    done(r4.at[:, pl.ds(0, nz - 1)], p3s.at[0])
    for i in range(5):
        done(lim_c, ms.at[i])


def body(groups, members, partials):
    shots, depth, lateral, width = partials.shape
    nd, nz, rows, cw = depth // groups, members // 2, lateral // members, width // 4
    parts = 4 if rows % 64 == 0 else 1
    rr, edge = rows // parts, min(8, rows)
    steps = 2 * nd * parts
    src = partials.reshape(2, 2, nd, nz, 2, rows, width)
    kind = partials.dtype
    dma = pltpu.SemaphoreType.DMA
    return pl.pallas_call(
        functools.partial(kernel, groups, members),
        out_shape=jax.ShapeDtypeStruct((nd, rows, width), F32),
        in_specs=[pl.BlockSpec(memory_space=pl.ANY)],
        out_specs=pl.BlockSpec(memory_space=pltpu.VMEM),
        scratch_shapes=[
            pltpu.VMEM((2, 2, nd, nz, 2, rows, width), kind),
            pltpu.VMEM((steps, 2, nz, 2, rr, 2 * cw), kind),
            pltpu.VMEM((steps, nz, 2, rr, cw), kind),
            pltpu.VMEM((steps, 2, nz, rr, cw), kind),
            pltpu.VMEM((steps, nz, 2, rr, cw), kind),
            pltpu.VMEM((steps, 2, nz, rr, cw), kind),
            pltpu.VMEM((2, steps, nz, rr, cw), kind),
            pltpu.VMEM((2, steps, nz, rr, cw), kind),
            pltpu.VMEM((steps, nz, rr, 2 * cw), F32),
            pltpu.VMEM((steps, nz, rr, 2 * cw), kind),
            pltpu.VMEM((steps, nz, rr, 2 * cw), kind),
            pltpu.VMEM((6, rr, cw), F32),
            pltpu.VMEM((rr, cw), F32),
            pltpu.VMEM((2, rr, cw), F32),
            pltpu.VMEM((2, rr, cw), F32),
            pltpu.VMEM((2, nz, rr, cw), F32),
            pltpu.VMEM((nd, rows, width), F32),
            pltpu.VMEM((rows, width), F32),
            pltpu.VMEM((rows, width), F32),
            pltpu.VMEM((nd, edge, width), F32),
            pltpu.VMEM((nd, edge, width), F32),
            dma((2 * nd,)),
            dma((1,)), dma((steps,)),
            dma((2,)), dma((2, steps)),
            dma((2,)), dma((2, steps)),
            dma((1,)), dma((steps,)),
            dma((5,)), dma((5,)),
            dma((2,)), dma((2,)),
            dma((4,)), dma((4,)),
        ],
        compiler_params=pltpu.CompilerParams(collective_id=0, has_side_effects=True),
    )(src)


def solution(mesh):
    groups, members = mesh.shape["shot"], mesh.shape["tile"]
    return jax.shard_map(
        functools.partial(body, groups, members),
        mesh=mesh,
        in_specs=(P(("shot", "tile"), None, None, None),),
        out_specs=P("shot", "tile", None),
        check_vma=False,
    )
```

time: 49.4 us -> 40.4 us (0.82)
  Pallas kernels: 47.5 us -> 38.5 us
    pallas_call x1, Pallas kernels: 47.5 us -> 38.5 us  [body(): pl.pallas_call(functools.partial(kernel, groups, members), out_shape=jax....]
where the time goes in v1:
time: 40.4 us; the launch traced here: 40.2 us
  Pallas kernels  38.5 us (95%)
  local copies, waits for them, and re-layouts  1.67 us (4%)
    pallas_call x1, Pallas kernels, body(): pl.pallas_call(functools.partial(kernel, groups, members), out_shape=jax....  38.5 us
    unnamed x1, local copies, waits for them, and re-layouts  1.67 us

profile of v1, /device:TPU:0, one launch (start us, length us, event | category | flops | bytes accessed | tf_op | source)
XLA Modules:
  0.0 40.2 jit_solution(16029995083190547909)
XLA Ops:
  0.0 38.5 %shard_map.17 = f32[2,64,512]{2,1,0:T(8,128)} custom-call(bf16[2,2,2,4,2,64,512]{6,5,4,3,2,1,0:T(8,128)(2,1)} %bitcast.1), custom_call_target="tpu_custom_call" | custom-call | tf_op jit(solution)/shard_map/pallas_call | solution.py:292
  38.6 1.7 %copy.3 = f32[2,64,512]{2,1,0:T(8,128)} copy(f32[2,64,512]{2,1,0:T(8,128)} %shard_map.17) | data formatting | bytes 524288

commit v2 on v1

--- a/solution.py
+++ b/solution.py
@@ -29,14 +29,20 @@
 
 
 def kernel(groups, members, src, out, own, rp, s1a, s1b, r1a, r1b, s2, r2, s3f, s3, r4,
-           lim, lim_c, lim_1, lim_2, lim_3, img, low, high, top, bottom, own_sem,
-           cs, cr, p1s, p1r, p2s, p2r, p3s, p3r, ms, mr, ns, nr, hs, hr):
+           sz, rz, tz, sw, rw, lim, lim_c, lim_1, lim_2, lim_3, lim_z, lim_w,
+           img, low, high, top, bottom, own_sem, cs, cr, p1s, p1r, p2s, p2r, p3s, p3r,
+           zs, zr, ws, wr, ms, mr, ns, nr, vs, vr, hs, hr, chain):
     nd, nz, rows, width = src.shape[2], src.shape[3], src.shape[5], src.shape[6]
     cw = width // 4
     rr = s2.shape[3]
     edge = top.shape[1]
     units = [(j, d, h) for d in range(nd) for h in range(0, rows, rr) for j in range(2)]
-    steps = len(units)
+    early = sz.shape[0]
+    at = len(units) * 5 // 8
+    late = units[at:at + early]
+    units = units[:at] + units[at + early:] + late
+    total_steps = len(units)
+    steps = total_steps - early
     g, t = lax.axis_index("shot"), lax.axis_index("tile")
     x, c = g // 2, g % 2
     z, y = t // 2, t % 2
@@ -47,6 +53,7 @@
     x_peer = dev((1 - x) * 2 + c, t)
     c_peer = dev(x * 2 + 1 - c, t)
     y_peer = dev(g, z * 2 + 1 - y)
+    d_peer = dev((1 - x) * 2 + c, z * 2 + 1 - y)
 
     def z_peer(o):
         return dev(g, lax.rem(z + o, nz) * 2 + y)
@@ -59,11 +66,12 @@
     ]
 
     barrier = pltpu.get_barrier_semaphore()
-    peers = [x_peer, c_peer, y_peer] + [z_peer(o) for o in range(1, nz)]
+    near = [(z > 0, dev(g, t - 2)), (z < nz - 1, dev(g, t + 2))]
+    peers = [c_peer, x_peer, y_peer]
     count = jnp.int32(len(peers))
     for peer in peers:
         pl.semaphore_signal(barrier, inc=1, device_id=peer, device_id_type=MESH)
-    for there, peer in beside:
+    for there, peer in near:
         count = count + jnp.where(there, 1, 0)
 
         @pl.when(there)
@@ -110,9 +118,24 @@
     for d in range(nd):
         loads[2 * d].wait()
     pl.semaphore_wait(barrier, count)
-    lead = min(4, steps)
-    for k in range(lead):
+    order = []
+    for k in range(steps):
+        order.append(k)
+        if k < early:
+            order.append(steps + k)
+    lead = min(4, len(order))
+    for k in order[:lead]:
         give(k)
+    for way, (there, peer) in enumerate([near[1], near[0]]):
+        behind = z if way == 0 else nz - 1 - z
+
+        @pl.when(behind > 1)
+        def _():
+            pl.semaphore_wait(chain.at[way], 1)
+
+        @pl.when(jnp.logical_and(there, behind > 0))
+        def _():
+            pl.semaphore_signal(chain.at[way], inc=1, device_id=peer, device_id_type=MESH)
     for d in range(nd):
         loads[2 * d + 1].wait()
 
@@ -133,7 +156,7 @@
     most = jnp.max(most, axis=1, keepdims=True)
     lim[0] = jnp.broadcast_to(jnp.maximum(most, TINY), (rr, cw))
     to_core = remote(lim.at[0], lim_c, ms.at[0], mr.at[0], c_peer)
-    for k in range(lead, steps):
+    for k in order[lead:]:
         give(k)
     to_core.wait_recv()
     lim[1] = lim[0] + lim_c[...]
@@ -141,6 +164,19 @@
     remote(lim.at[1], lim_1.at[1], ms.at[2], mr.at[2], y_peer)
 
     def limits(stage):
+        if stage == 1 and early:
+            for o in range(1, nz):
+                remote(lim.at[1], lim_z.at[z], vs.at[0], vr.at[0], z_peer(o))
+        if stage == 5 and early:
+            done(lim_z.at[pl.ds(0, nz - 1)], vr.at[0])
+            most = lim[1]
+            for o in range(1, nz):
+                most = most + lim_z[lax.rem(z + o, nz)]
+            lim[6] = most
+            for i, peer in enumerate([d_peer, x_peer, y_peer]):
+                remote(lim.at[6], lim_w.at[i], vs.at[1], vr.at[1], peer)
+        if stage == 6 and early:
+            done(lim_w, vr.at[1])
         if stage == 2:
             for kind, peer in enumerate([y_peer, x_peer]):
                 done(lim_1.at[kind], mr.at[1 + kind])
@@ -200,6 +236,41 @@
             copies.append(remote(s3.at[k, to], r4.at[k, z], p3s.at[0], p3r.at[k], z_peer(o)))
         third[k] = copies
 
+    def z1(i):
+        k = steps + i
+        pair[k].wait_recv()
+        scale = jnp.concatenate([up(lim[1])] * 2, axis=-1)
+        d, r, w = span(k)
+        for o in range(1, nz):
+            to = lax.rem(z + o, nz)
+            for a in range(2):
+                sz[i, to, a] = encode(own[a, c, d, to, :, r, w].astype(F32) + rp[k, a, to].astype(F32), scale)
+            remote(sz.at[i, to], rz.at[i, z], zs.at[0], zr.at[i], z_peer(o))
+
+    def z2(i):
+        k = steps + i
+        done(rz.at[i, pl.ds(0, nz - 1)], zr.at[i])
+        d, r, w = span(k)
+        scale = jnp.concatenate([up(lim[6])] * 2, axis=-1)
+        for a in range(2):
+            total = own[a, c, d, z, :, r, w].astype(F32) + rp[k, a, z].astype(F32)
+            for o in range(1, nz):
+                of = lax.rem(z + o, nz)
+                total = total + decode(rz[i, of, a], jnp.concatenate([down(lim_z[of])] * 2, axis=-1))
+            tz[i, a] = total
+            sw[i, a] = encode(total, scale)
+        for n, (a, b, peer) in enumerate([(1 - x, 1 - y, d_peer), (1 - x, y, x_peer), (x, 1 - y, y_peer)]):
+            remote(sw.at[i, a, b], rw.at[i, n], ws.at[0], wr.at[i], peer)
+
+    def z3(i):
+        done(rw.at[i], wr.at[i])
+        total = tz[i, x, y]
+        for n in range(3):
+            total = total + decode(rw[i, n], jnp.concatenate([lim_w[n] * (1.0 / TOP)] * 2, axis=-1))
+        _, r, w = span(steps + i)
+        img[units[steps + i][1], r, w] = total * shrink
+        edges(steps + i)
+
     shrink = 1.0 / jnp.sqrt(F32(groups * members))
 
     def halo(side, a, b):
@@ -220,6 +291,11 @@
                 at = lax.rem(z + nz - o, nz)
                 total = total + decode(r4[k, at, :, lanes], lim_3[kind, at] * (1.0 / TOP))
             img[d, r, kind_cols(kind, k)] = total * shrink
+        edges(k)
+
+    def edges(k):
+        j, d, h = units[k]
+        _, r, w = span(k)
         if d == 0:
             halo(0, img.at[d, r, w], high.at[r, w])
         if d == nd - 1:
@@ -229,9 +305,16 @@
         if h + rr == rows:
             halo(3, img.at[d, pl.ds(rows - edge, edge), w], top.at[d, :, w])
 
-    ahead, lag3, lag4 = 3, 2, 5
-    for k in range(min(ahead, steps)):
+    ahead, lag3, lag4, at_z2 = 5, 6, 11, 9
+    ahead = min(ahead, steps)
+    p1(0)
+    limits(1)
+    for k in range(1, ahead):
+        if k <= early:
+            z1(k - 1)
         p1(k)
+    for i in range(max(ahead - 1, 0), early):
+        z1(i)
     limits(2)
     for k in range(steps + lag4):
         if k < steps:
@@ -240,10 +323,18 @@
             p1(k + ahead)
         if k == min(1, steps - 1):
             limits(3)
+        if k == min(at_z2, steps - 1):
+            limits(5)
+            for i in range(early):
+                z2(i)
         if 0 <= k - lag3 < steps:
             p3(k - lag3)
         if k == lag4:
             limits(4)
+        if k == steps + lag4 - 2:
+            limits(6)
+            for i in range(early):
+                z3(i)
         if 0 <= k - lag4 < steps:
             last(k - lag4)
     for side, ref in enumerate([high, low, bottom, top]):
@@ -276,6 +367,11 @@
         done(r2.at[kind], p2s.at[kind])
         done(lim_3.at[kind, pl.ds(0, nz - 1)], ns.at[kind])
     done(r4.at[:, pl.ds(0, nz - 1)], p3s.at[0])
+    if early:
+        done(rz.at[:, pl.ds(0, nz - 1)], zs.at[0])
+        done(rw, ws.at[0])
+        done(lim_z.at[pl.ds(0, nz - 1)], vs.at[0])
+        done(lim_w, vs.at[1])
     for i in range(5):
         done(lim_c, ms.at[i])
 
@@ -285,7 +381,9 @@
     nd, nz, rows, cw = depth // groups, members // 2, lateral // members, width // 4
     parts = 4 if rows % 64 == 0 else 1
     rr, edge = rows // parts, min(8, rows)
-    steps = 2 * nd * parts
+    early = 3 if parts > 1 else 1
+    total = 2 * nd * parts
+    steps = total - early
     src = partials.reshape(2, 2, nd, nz, 2, rows, width)
     kind = partials.dtype
     dma = pltpu.SemaphoreType.DMA
@@ -296,7 +394,7 @@
         out_specs=pl.BlockSpec(memory_space=pltpu.VMEM),
         scratch_shapes=[
             pltpu.VMEM((2, 2, nd, nz, 2, rows, width), kind),
-            pltpu.VMEM((steps, 2, nz, 2, rr, 2 * cw), kind),
+            pltpu.VMEM((total, 2, nz, 2, rr, 2 * cw), kind),
             pltpu.VMEM((steps, nz, 2, rr, cw), kind),
             pltpu.VMEM((steps, 2, nz, rr, cw), kind),
             pltpu.VMEM((steps, nz, 2, rr, cw), kind),
@@ -306,26 +404,37 @@
             pltpu.VMEM((steps, nz, rr, 2 * cw), F32),
             pltpu.VMEM((steps, nz, rr, 2 * cw), kind),
             pltpu.VMEM((steps, nz, rr, 2 * cw), kind),
-            pltpu.VMEM((6, rr, cw), F32),
+            pltpu.VMEM((early, nz, 2, 2, rr, 2 * cw), kind),
+            pltpu.VMEM((early, nz, 2, 2, rr, 2 * cw), kind),
+            pltpu.VMEM((early, 2, 2, rr, 2 * cw), F32),
+            pltpu.VMEM((early, 2, 2, rr, 2 * cw), kind),
+            pltpu.VMEM((early, 3, rr, 2 * cw), kind),
+            pltpu.VMEM((7, rr, cw), F32),
             pltpu.VMEM((rr, cw), F32),
             pltpu.VMEM((2, rr, cw), F32),
             pltpu.VMEM((2, rr, cw), F32),
             pltpu.VMEM((2, nz, rr, cw), F32),
+            pltpu.VMEM((nz, rr, cw), F32),
+            pltpu.VMEM((3, rr, cw), F32),
             pltpu.VMEM((nd, rows, width), F32),
             pltpu.VMEM((rows, width), F32),
             pltpu.VMEM((rows, width), F32),
             pltpu.VMEM((nd, edge, width), F32),
             pltpu.VMEM((nd, edge, width), F32),
             dma((2 * nd,)),
-            dma((1,)), dma((steps,)),
+            dma((1,)), dma((total,)),
             dma((2,)), dma((2, steps)),
             dma((2,)), dma((2, steps)),
             dma((1,)), dma((steps,)),
+            dma((1,)), dma((early,)),
+            dma((1,)), dma((early,)),
             dma((5,)), dma((5,)),
             dma((2,)), dma((2,)),
+            dma((2,)), dma((2,)),
             dma((4,)), dma((4,)),
+            pltpu.SemaphoreType.REGULAR((2,)),
         ],
-        compiler_params=pltpu.CompilerParams(collective_id=0, has_side_effects=True),
+        compiler_params=pltpu.CompilerParams(collective_id=0, has_side_effects=True, vmem_limit_bytes=51 * 2**20),
     )(src)
 
 

time: 40.4 us -> 34.6 us (0.86)
  Pallas kernels: 38.5 us -> 33.7 us
  local copies, waits for them, and re-layouts: 1.67 us -> 0.71 us
    pallas_call x1, Pallas kernels: 38.5 us -> 33.7 us  [body(): pl.pallas_call(functools.partial(kernel, groups, members), out_shape=jax....]
    unnamed x1, local copies, waits for them, and re-layouts: 1.67 us -> 0.71 us
where the time goes in v2:
time: 34.6 us; the launch traced here: 34.4 us
  Pallas kernels  33.7 us (97%)
  local copies, waits for them, and re-layouts  0.71 us (2%)
    pallas_call x1, Pallas kernels, body(): pl.pallas_call(functools.partial(kernel, groups, members), out_shape=jax....  33.7 us
    unnamed x1, local copies, waits for them, and re-layouts  0.71 us

profile of v2, /device:TPU:0, one launch (start us, length us, event | category | flops | bytes accessed | tf_op | source)
XLA Modules:
  0.0 34.4 jit_solution(12460870667863627708)
XLA Ops:
  0.0 33.7 %shard_map.17 = f32[2,64,512]{2,1,0:T(8,128)S(1)} custom-call(bf16[2,2,2,4,2,64,512]{6,5,4,3,2,1,0:T(8,128)(2,1)} %bitcast.1), custom_call_target="tpu_custom_call" | custom-call | tf_op jit(solution)/shard_map/pallas_call | solution.py:390
  33.7 0.7 %copy.3 = f32[2,64,512]{2,1,0:T(8,128)} copy(f32[2,64,512]{2,1,0:T(8,128)S(1)} %shard_map.17) | data formatting | bytes 524288

commit v3 on v2

--- a/solution.py
+++ b/solution.py
@@ -11,6 +11,31 @@
 F32 = jnp.float32
 TOP = 180.0
 TINY = 1e-30
+
+
+def plan(steps, early):
+    ahead, lag3, lag4, at_b, at_c = 5, 7, 12, 9, 2
+    ahead = min(ahead, steps)
+    seq = []
+    for k in range(ahead):
+        seq.append(("1", k))
+        if 1 <= k <= early:
+            seq.append(("A", k - 1))
+    seq += [("A", k) for k in range(max(ahead - 1, 0), early)]
+    for k in range(steps + lag4):
+        if k < steps:
+            seq.append(("2", k))
+        if k + ahead < steps:
+            seq.append(("1", k + ahead))
+        if k == min(at_b, steps - 1):
+            seq += [("B", i) for i in range(early)]
+        if 0 <= k - lag3 < steps:
+            seq.append(("3", k - lag3))
+        if k == steps + lag4 - at_c:
+            seq += [("C", i) for i in range(early)]
+        if 0 <= k - lag4 < steps:
+            seq.append(("4", k - lag4))
+    return seq
 
 
 def encode(value, scale):
@@ -115,42 +140,28 @@
         lanes = pl.ds(kind * cw, cw)
         return own[a, c, d, :, b, r, kind_cols(kind, k)].astype(F32) + rp[k, a, :, b, :, lanes].astype(F32)
 
-    for d in range(nd):
-        loads[2 * d].wait()
-    pl.semaphore_wait(barrier, count)
     order = []
     for k in range(steps):
         order.append(k)
-        if k < early:
-            order.append(steps + k)
-    lead = min(4, len(order))
-    for k in order[:lead]:
-        give(k)
-    for way, (there, peer) in enumerate([near[1], near[0]]):
-        behind = z if way == 0 else nz - 1 - z
-
-        @pl.when(behind > 1)
-        def _():
-            pl.semaphore_wait(chain.at[way], 1)
-
-        @pl.when(jnp.logical_and(there, behind > 0))
-        def _():
-            pl.semaphore_signal(chain.at[way], inc=1, device_id=peer, device_id_type=MESH)
+        if 1 <= k <= early:
+            order.append(steps + k - 1)
+    lead = 2
+    most = jnp.zeros((rr, width), own.dtype)
     for d in range(nd):
-        loads[2 * d + 1].wait()
-
-    most = None
-    for a in range(2):
-        for b in range(2):
-            for d in range(nd):
-                def step(i, most, a=a, b=b, d=d):
-                    for e in range(2):
-                        block = jnp.abs(own[a, b, d, i, e])
+        for core in range(2):
+            loads[2 * d + core].wait()
+            if d == 0 and core == 0:
+                pl.semaphore_wait(barrier, count)
+                for k in order[:lead]:
+                    give(k)
+            at = 1 - c if core == 0 else c
+            for a in range(2):
+                def step(i, most, a=a, at=at, d=d):
+                    for b in range(2):
+                        block = jnp.abs(own[a, at, d, i, b])
                         for r in range(0, rows, rr):
                             most = jnp.maximum(most, block[r:r + rr])
                     return most
-                if most is None:
-                    most = jnp.zeros((rr, width), own.dtype)
                 most = lax.fori_loop(0, nz, step, most)
     most = jnp.max(most.astype(F32), axis=0, keepdims=True)
     most = jnp.max(most, axis=1, keepdims=True)
@@ -164,10 +175,10 @@
     remote(lim.at[1], lim_1.at[1], ms.at[2], mr.at[2], y_peer)
 
     def limits(stage):
-        if stage == 1 and early:
+        if stage == "A":
             for o in range(1, nz):
                 remote(lim.at[1], lim_z.at[z], vs.at[0], vr.at[0], z_peer(o))
-        if stage == 5 and early:
+        if stage == "B":
             done(lim_z.at[pl.ds(0, nz - 1)], vr.at[0])
             most = lim[1]
             for o in range(1, nz):
@@ -175,20 +186,20 @@
             lim[6] = most
             for i, peer in enumerate([d_peer, x_peer, y_peer]):
                 remote(lim.at[6], lim_w.at[i], vs.at[1], vr.at[1], peer)
-        if stage == 6 and early:
+        if stage == "C":
             done(lim_w, vr.at[1])
-        if stage == 2:
+        if stage == "2":
             for kind, peer in enumerate([y_peer, x_peer]):
                 done(lim_1.at[kind], mr.at[1 + kind])
                 lim[2 + kind] = lim[1] + lim_1[kind]
                 remote(lim.at[2 + kind], lim_2.at[kind], ms.at[3 + kind], mr.at[3 + kind], peer)
-        if stage == 3:
+        if stage == "3":
             for kind in range(2):
                 done(lim_2.at[kind], mr.at[3 + kind])
                 lim[4 + kind] = lim[2 + kind] + lim_2[kind]
                 for o in range(1, nz):
                     remote(lim.at[4 + kind], lim_3.at[kind, z], ns.at[kind], nr.at[kind], z_peer(o))
-        if stage == 4:
+        if stage == "4":
             for kind in range(2):
                 done(lim_3.at[kind, pl.ds(0, nz - 1)], nr.at[kind])
 
@@ -305,57 +316,54 @@
         if h + rr == rows:
             halo(3, img.at[d, pl.ds(rows - edge, edge), w], top.at[d, :, w])
 
-    ahead, lag3, lag4, at_z2 = 5, 6, 11, 9
-    ahead = min(ahead, steps)
-    p1(0)
-    limits(1)
-    for k in range(1, ahead):
-        if k <= early:
-            z1(k - 1)
-        p1(k)
-    for i in range(max(ahead - 1, 0), early):
-        z1(i)
-    limits(2)
-    for k in range(steps + lag4):
-        if k < steps:
-            p2(k)
-        if k + ahead < steps:
-            p1(k + ahead)
-        if k == min(1, steps - 1):
-            limits(3)
-        if k == min(at_z2, steps - 1):
-            limits(5)
-            for i in range(early):
-                z2(i)
-        if 0 <= k - lag3 < steps:
-            p3(k - lag3)
-        if k == lag4:
-            limits(4)
-        if k == steps + lag4 - 2:
-            limits(6)
-            for i in range(early):
-                z3(i)
-        if 0 <= k - lag4 < steps:
-            last(k - lag4)
-    for side, ref in enumerate([high, low, bottom, top]):
-        @pl.when(beside[side ^ 1][0])
-        def _():
-            done(ref, hr.at[side])
-
+    def greet():
+        for way, (there, peer) in enumerate([near[1], near[0]]):
+            behind = z if way == 0 else nz - 1 - z
+
+            @pl.when(behind > 1)
+            def _():
+                pl.semaphore_wait(chain.at[way], 1)
+
+            @pl.when(jnp.logical_and(there, behind > 0))
+            def _():
+                pl.semaphore_signal(chain.at[way], inc=1, device_id=peer, device_id_type=MESH)
+
+    run = {"1": p1, "2": p2, "3": p3, "4": last, "A": z1, "B": z2, "C": z3}
+    begun = set()
+    for op, k in plan(steps, early):
+        if op not in begun:
+            begun.add(op)
+            if op in "A3" and "greet" not in begun:
+                begun.add("greet")
+                greet()
+            limits(op)
+        run[op](k)
     rown = lax.broadcasted_iota(jnp.int32, (rows, width), 0)
     coln = lax.broadcasted_iota(jnp.int32, (rows, width), 1)
+
+    def arrive(sides):
+        for side in sides:
+            @pl.when(beside[side ^ 1][0])
+            def _():
+                done([high, low, bottom, top][side], hr.at[side])
+
+    arrive([2, 3])
     for d in range(nd):
         here = img[d]
-        below = img[d - 1] if d > 0 else jnp.where(g > 0, low[...], 0.0)
-        above = img[d + 1] if d < nd - 1 else jnp.where(g < groups - 1, high[...], 0.0)
         before = jnp.where(t > 0, top[d, edge - 1:edge, :], 0.0)
         after = jnp.where(t < members - 1, bottom[d, 0:1, :], 0.0)
-        near = above + below
-        near = near + jnp.where(rown == rows - 1, after, pltpu.roll(here, rows - 1, 0))
+        near = jnp.where(rown == rows - 1, after, pltpu.roll(here, rows - 1, 0))
         near = near + jnp.where(rown == 0, before, pltpu.roll(here, 1, 0))
         near = near + jnp.where(coln == width - 1, 0.0, pltpu.roll(here, width - 1, 1))
         near = near + jnp.where(coln == 0, 0.0, pltpu.roll(here, 1, 1))
+        if d > 0:
+            near = near + img[d - 1]
+        if d < nd - 1:
+            near = near + img[d + 1]
         out[d] = 6.0 * here - near
+    arrive([0, 1])
+    out[0] = out[0] - jnp.where(g > 0, low[...], 0.0)
+    out[nd - 1] = out[nd - 1] - jnp.where(g < groups - 1, high[...], 0.0)
     for side, ref in enumerate([high, low, bottom, top]):
         @pl.when(beside[side][0])
         def _():

time: 34.6 us -> 34 us (0.983); the launches traced: 34.4 us -> 33.4 us
  Pallas kernels: 33.7 us -> 32.7 us
    pallas_call x1, Pallas kernels: 33.7 us -> 32.7 us  [body(): pl.pallas_call(functools.partial(kernel, groups, members), out_shape=jax....]
where the time goes in v3:
time: 34 us; the launch traced here: 33.4 us
  Pallas kernels  32.7 us (96%)
  local copies, waits for them, and re-layouts  0.71 us (2%)
    pallas_call x1, Pallas kernels, body(): pl.pallas_call(functools.partial(kernel, groups, members), out_shape=jax....  32.7 us
    unnamed x1, local copies, waits for them, and re-layouts  0.71 us

profile of v3, /device:TPU:0, one launch (start us, length us, event | category | flops | bytes accessed | tf_op | source)
XLA Modules:
  0.0 33.4 jit_solution(16419134329303142270)
XLA Ops:
  0.0 32.7 %shard_map.17 = f32[2,64,512]{2,1,0:T(8,128)S(1)} custom-call(bf16[2,2,2,4,2,64,512]{6,5,4,3,2,1,0:T(8,128)(2,1)} %bitcast.1), custom_call_target="tpu_custom_call" | custom-call | tf_op jit(solution)/shard_map/pallas_call | solution.py:398
  32.7 0.7 %copy.3 = f32[2,64,512]{2,1,0:T(8,128)} copy(f32[2,64,512]{2,1,0:T(8,128)S(1)} %shard_map.17) | data formatting | bytes 524288

commit v4 on v3

--- a/solution.py
+++ b/solution.py
@@ -14,27 +14,30 @@
 
 
 def plan(steps, early):
-    ahead, lag3, lag4, at_b, at_c = 5, 7, 12, 9, 2
+    ahead, lag, single, least, before, at_b = 5, 6, 0, 4, 2, 11
     ahead = min(ahead, steps)
+    third = [max(k + least, lag + min(k, single) + max(k - single, 0) // 2) for k in range(steps)]
     seq = []
     for k in range(ahead):
         seq.append(("1", k))
         if 1 <= k <= early:
             seq.append(("A", k - 1))
     seq += [("A", k) for k in range(max(ahead - 1, 0), early)]
-    for k in range(steps + lag4):
+    ends = list(range(steps))
+    for k in range(third[-1] + 1):
         if k < steps:
             seq.append(("2", k))
         if k + ahead < steps:
             seq.append(("1", k + ahead))
         if k == min(at_b, steps - 1):
             seq += [("B", i) for i in range(early)]
-        if 0 <= k - lag3 < steps:
-            seq.append(("3", k - lag3))
-        if k == steps + lag4 - at_c:
-            seq += [("C", i) for i in range(early)]
-        if 0 <= k - lag4 < steps:
-            seq.append(("4", k - lag4))
+        seq += [("3", i) for i in range(steps) if third[i] == k]
+        if third[-1] - before <= k < third[-1] and third[ends[0]] < k:
+            seq.append(("4", ends.pop(0)))
+    for i in ends:
+        if i == ends[-2 if len(ends) > 1 else -1]:
+            seq += [("C", j) for j in range(early)]
+        seq.append(("4", i))
     return seq
 
 
@@ -389,7 +392,7 @@
     nd, nz, rows, cw = depth // groups, members // 2, lateral // members, width // 4
     parts = 4 if rows % 64 == 0 else 1
     rr, edge = rows // parts, min(8, rows)
-    early = 3 if parts > 1 else 1
+    early = 2 if parts > 1 else 1
     total = 2 * nd * parts
     steps = total - early
     src = partials.reshape(2, 2, nd, nz, 2, rows, width)

time: 34 us -> 32.8 us (0.965); the launches traced: 33.4 us -> 32.7 us
  Pallas kernels: 32.7 us -> 31.9 us
    pallas_call x1, Pallas kernels: 32.7 us -> 31.9 us  [body(): pl.pallas_call(functools.partial(kernel, groups, members), out_shape=jax....]
where the time goes in v4:
time: 32.8 us; the launch traced here: 32.7 us
  Pallas kernels  31.9 us (97%)
  local copies, waits for them, and re-layouts  0.71 us (2%)
    pallas_call x1, Pallas kernels, body(): pl.pallas_call(functools.partial(kernel, groups, members), out_shape=jax....  31.9 us
    unnamed x1, local copies, waits for them, and re-layouts  0.71 us

profile of v4, /device:TPU:0, one launch (start us, length us, event | category | flops | bytes accessed | tf_op | source)
XLA Modules:
  0.0 32.7 jit_solution(16697288963727892817)
XLA Ops:
  0.0 31.9 %shard_map.17 = f32[2,64,512]{2,1,0:T(8,128)S(1)} custom-call(bf16[2,2,2,4,2,64,512]{6,5,4,3,2,1,0:T(8,128)(2,1)} %bitcast.1), custom_call_target="tpu_custom_call" | custom-call | tf_op jit(solution)/shard_map/pallas_call | solution.py:401
  32.0 0.7 %copy.3 = f32[2,64,512]{2,1,0:T(8,128)} copy(f32[2,64,512]{2,1,0:T(8,128)S(1)} %shard_map.17) | data formatting | bytes 524288

commit v5 on v4

--- a/solution.py
+++ b/solution.py
@@ -65,6 +65,7 @@
     rr = s2.shape[3]
     edge = top.shape[1]
     units = [(j, d, h) for d in range(nd) for h in range(0, rows, rr) for j in range(2)]
+    units = sorted(units, key=lambda unit: 0 < unit[2] < rows - rr)
     early = sz.shape[0]
     at = len(units) * 5 // 8
     late = units[at:at + early]

time: 32.8 us -> 32.3 us (0.985)
  Pallas kernels: 31.9 us -> 31.4 us
    pallas_call x1, Pallas kernels: 31.9 us -> 31.4 us  [body(): pl.pallas_call(functools.partial(kernel, groups, members), out_shape=jax....]
where the time goes in v5:
time: 32.3 us; the launch traced here: 32.1 us
  Pallas kernels  31.4 us (97%)
  local copies, waits for them, and re-layouts  0.71 us (2%)
    pallas_call x1, Pallas kernels, body(): pl.pallas_call(functools.partial(kernel, groups, members), out_shape=jax....  31.4 us
    unnamed x1, local copies, waits for them, and re-layouts  0.71 us

profile of v5, /device:TPU:0, one launch (start us, length us, event | category | flops | bytes accessed | tf_op | source)
XLA Modules:
  0.0 32.1 jit_solution(3922976601248789151)
XLA Ops:
  0.0 31.4 %shard_map.17 = f32[2,64,512]{2,1,0:T(8,128)S(1)} custom-call(bf16[2,2,2,4,2,64,512]{6,5,4,3,2,1,0:T(8,128)(2,1)} %bitcast.1), custom_call_target="tpu_custom_call" | custom-call | tf_op jit(solution)/shard_map/pallas_call | solution.py:402
  31.4 0.7 %copy.3 = f32[2,64,512]{2,1,0:T(8,128)} copy(f32[2,64,512]{2,1,0:T(8,128)S(1)} %shard_map.17) | data formatting | bytes 524288
